TPU v7x, 32 devices: a whole 2x2x4 slice. The times are simulated.
32 devices in a mesh: aa: 2 (over y), ba: 4 (over x, core), col: 4 (over z).
Axes of the slice: x: 2, y: 2, z: 4, core: 2. Of those that a mesh axis runs over, the one named last changes fastest.
Arguments:
- hidden: bfloat16 [2, 4, 32, 8192], P('aa', 'ba', None, 'col'), may hold values from -36 to 60, as said below
- unembed: bfloat16 [8192, 152064], P(None, ('aa', 'ba', 'col')), may hold values from -1 to 5, as said below
- targets: int32 [2, 4, 32], replicated, may hold values from 0 to 152063
- lengths: int32 [2, 4], replicated, may hold values from 1 to 32
Outputs:
- scores: float32 [2, 4], P('aa', 'ba')
Inputs may be any that keep to these rules, and one draw needn't show every extreme that they name: real-valued hidden states. `unembed`: real-valued unembedding entries.
All inputs are finite; a program needn't handle non-finite values.
Results may differ from a plain program's by a relative error of at most 0.0003.
Values may be sent and summed in bfloat16 or wider, within the bound.
A program may use at most 128 MiB of HBM per device.

v0:
```python
import functools
import math

import jax
import jax.numpy as jnp
from jax import lax
from jax.experimental import pallas as pl
from jax.experimental.pallas import tpu as pltpu
from jax.sharding import PartitionSpec as P

MESH = pl.DeviceIdType.MESH
VMEM_BUDGET = 59 * 2**20
Z, X, A, DIAG, SIB = range(5)


def round_up(value, to):
    return (value + to - 1) // to * to


def flip(value, step, count):
    if count & (count - 1):
        return lax.rem(value + step, count)
    bit = 1
    while bit < count:
        on = lax.rem(step // bit, 2)
        value = value + on * (bit - 2 * bit * lax.rem(value // bit, 2))
        bit *= 2
    return value


def kernel(dims, hid_ref, w_ref, tgt_ref, len_ref, out_ref, hid, wbuf, acc, stat_send, stat_recv,
           own_sem, w_sem, recv_sem, plane_sem, z_sem, stat_send_sem, stat_recv_sem):
    n_a, n_b, n_c, rows, width, vocab, tile, slots = dims
    n_x = n_b // 2
    groups = n_a * n_b
    n_dev = groups * n_c
    chunks = hid_ref.shape[1] // width
    units = n_c * chunks
    a, b, c = lax.axis_index("aa"), lax.axis_index("ba"), lax.axis_index("col")
    x, k = b // 2, lax.rem(b, 2)
    rank = a * n_b + b
    me = rank * n_c + c

    def unit_of(i):
        return flip(c, i // chunks, n_c) * chunks + lax.rem(i, chunks)

    def block(u, r, count=1):
        return hid.at[u, pl.ds(pl.multiple_of(r * rows, rows), rows * count), :]

    def weights(i):
        start = pl.multiple_of(unit_of(i) * width, width)
        slot = lax.rem(i, slots)
        return pltpu.make_async_copy(w_ref.at[:, pl.ds(start, width)], wbuf.at[slot], w_sem.at[slot])

    def own(j):
        return pltpu.make_async_copy(
            hid_ref.at[:, pl.ds(j * width, width)], block(c * chunks + j, rank), own_sem.at[j])

    def send(u, r, kind, device, sem):
        pltpu.make_async_remote_copy(
            src_ref=block(u, r), dst_ref=block(u, r), send_sem=sem, recv_sem=recv_sem.at[kind, u],
            device_id=device, device_id_type=MESH).start()

    def await_blocks(u, kind, count):
        if count:
            ref = block(u, 0, count)
            pltpu.make_async_copy(ref, ref, recv_sem.at[kind, u]).wait()

    def to_sibling(u, r):
        send(u, r, SIB, (a, b + 1 - 2 * k, c), plane_sem.at[u])

    def share(u):
        for dx in range(1, n_x):
            send(u, rank, X, (a, lax.rem(x + dx, n_x) * 2 + k, c), plane_sem.at[u])
        for da in range(1, n_a):
            send(u, rank, A, (lax.rem(a + da, n_a), b, c), plane_sem.at[u])
        to_sibling(u, rank)

    def stage0(i):
        u = unit_of(i)
        await_blocks(u, Z, 1)
        share(u)

    def stage1(i):
        u = unit_of(i)
        await_blocks(u, X, n_x - 1)
        await_blocks(u, A, n_a - 1)
        for da in range(1, n_a):
            for dx in range(1, n_x):
                step_a = lax.rem(a + da, n_a) - a
                step_x = lax.rem(x + dx, n_x) - x
                src = (a + step_a * (1 - k)) * n_b + (x + step_x * k) * 2 + k
                send(u, src, DIAG, (a + step_a * k, (x + step_x * (1 - k)) * 2 + k, c), plane_sem.at[u])
        for dx in range(1, n_x):
            to_sibling(u, a * n_b + lax.rem(x + dx, n_x) * 2 + k)
        for da in range(1, n_a):
            to_sibling(u, lax.rem(a + da, n_a) * n_b + b)

    def stage2(i):
        u = unit_of(i)
        await_blocks(u, DIAG, (n_a - 1) * (n_x - 1))
        for da in range(1, n_a):
            for dx in range(1, n_x):
                to_sibling(u, lax.rem(a + da, n_a) * n_b + lax.rem(x + dx, n_x) * 2 + k)

    for j in range(chunks):
        own(j).start()
    for i in range(slots):
        weights(i).start()

    def other(d):
        dev = lax.rem(me + d, n_dev)
        group = dev // n_c
        return (group // n_b, lax.rem(group, n_b), lax.rem(dev, n_c)), group

    barrier = pltpu.get_barrier_semaphore()

    @pl.loop(1, n_dev)
    def _(d):
        pl.semaphore_signal(barrier, inc=1, device_id=other(d)[0], device_id_type=MESH)

    for j in range(chunks):
        own(j).wait()
    pl.semaphore_wait(barrier, n_dev - 1)

    for j in range(chunks):
        share(c * chunks + j)
    for step in range(1, n_c):
        for j in range(chunks):
            u = c * chunks + j
            send(u, rank, Z, (a, b, flip(c, step, n_c)), z_sem.at[j])

    acc[...] = jnp.zeros_like(acc)
    stat_send[...] = jnp.zeros_like(stat_send)

    lead0, lead1, lead2 = 3, 2, 1
    for i in range(lead1):
        if i >= chunks:
            stage0(i)
        stage1(i)
        if i == 0:
            stage2(0)
    for i in range(max(chunks, lead1), lead0):
        stage0(i)

    def accumulate(u, slot, span):
        acc[span, :] += lax.dot_general(
            wbuf[slot, span, :], hid[u], (((1,), (1,)), ((), ())), preferred_element_type=jnp.float32)

    @pl.loop(0, units)
    def _(i):
        @pl.when(jnp.logical_and(i + lead0 >= chunks, i + lead0 < units))
        def _():
            stage0(i + lead0)

        @pl.when(i + lead1 < units)
        def _():
            stage1(i + lead1)

        @pl.when(i + lead2 < units)
        def _():
            stage2(i + lead2)

        u = unit_of(i)
        await_blocks(u, SIB, groups // 2)
        weights(i).wait()
        slot = lax.rem(i, slots)

        @pl.loop(0, vocab // tile)
        def _(n):
            accumulate(u, slot, pl.ds(pl.multiple_of(n * tile, 8), tile))

        if vocab % tile:
            accumulate(u, slot, pl.ds(vocab // tile * tile, vocab % tile))

        @pl.when(i + slots < units)
        def _():
            weights(i + slots).start()

    ids = jnp.concatenate(
        [tgt_ref[g // n_b, g % n_b:g % n_b + 1, :] for g in range(groups)], axis=1) - me * vocab
    for t in range(groups * rows // 128):
        lanes = slice(t * 128, (t + 1) * 128)
        part = acc[:, lanes]
        top = jnp.max(part, axis=0, keepdims=True)
        at = lax.broadcasted_iota(jnp.int32, part.shape, 0)
        stat_send[t, 0:1, :] = top
        stat_send[t, 1:2, :] = jnp.sum(jnp.exp(part - top), axis=0, keepdims=True)
        stat_send[t, 2:3, :] = jnp.sum(jnp.where(at == ids[:, lanes], part, 0.0), axis=0, keepdims=True)

    def stats(d):
        device, group = other(d)
        return pltpu.make_async_remote_copy(
            src_ref=stat_send.at[group * rows // 128], dst_ref=stat_recv.at[me],
            send_sem=stat_send_sem, recv_sem=stat_recv_sem, device_id=device, device_id_type=MESH)

    @pl.loop(1, n_dev)
    def _(d):
        stats(d).start()

    stat_recv[me] = stat_send[rank * rows // 128]

    for u in range(units):
        ref = block(u, 0, groups - 1)
        pltpu.make_async_copy(ref, ref, plane_sem.at[u]).wait()
    if n_c > 1:
        for j in range(chunks):
            ref = hid.at[pl.ds(0, n_c - 1), 0:rows, :]
            pltpu.make_async_copy(ref, ref, z_sem.at[j]).wait()

    ref = stat_recv.at[pl.ds(0, n_dev - 1)]
    pltpu.make_async_copy(ref, ref, stat_recv_sem).wait()
    tops = stat_recv[:, 0:1, :]
    top = jnp.max(tops, axis=0, keepdims=True)
    total = jnp.sum(stat_recv[:, 1:2, :] * jnp.exp(tops - top), axis=0)
    picked = jnp.sum(stat_recv[:, 2:3, :], axis=0)
    logprob = picked - top[0] - jnp.log(total)
    live = len_ref[a, b]
    position = lax.broadcasted_iota(jnp.int32, logprob.shape, 1) - lax.rem(rank * rows, 128)
    valid = jnp.logical_and(position >= 0, position < live)
    summed = jnp.sum(jnp.where(valid, logprob, 0.0), axis=1, keepdims=True)
    out_ref[...] = summed / jnp.full((1, 1), live, jnp.int32).astype(jnp.float32)
    ref = stat_recv.at[pl.ds(0, n_dev - 1)]
    pltpu.make_async_copy(ref, ref, stat_send_sem).wait()


def body(hidden, unembed, targets, lengths):
    n_a, n_b, n_c = (lax.axis_size(name) for name in ("aa", "ba", "col"))
    rows = hidden.shape[0] * hidden.shape[1] * hidden.shape[2]
    part = hidden.shape[3]
    vocab = unembed.shape[1]
    width = math.gcd(part, 1024)
    chunks = part // width
    units = n_c * chunks
    groups = n_a * n_b
    n_dev = groups * n_c
    padded = round_up(vocab, 8)
    tile = max(t for t in range(8, min(vocab, 800) + 1, 8) if vocab % 8 or vocab % t == 0)
    held = groups * rows * (units * width * 2 + padded * 4) + (n_dev + groups) * 4096
    slots = min(units, (VMEM_BUDGET - held) // (width * padded * 2))
    dims = (n_a, n_b, n_c, rows, width, vocab, tile, slots)
    return pl.pallas_call(
        functools.partial(kernel, dims),
        out_shape=jax.ShapeDtypeStruct((1, 1), jnp.float32),
        in_specs=[
            pl.BlockSpec(memory_space=pl.ANY),
            pl.BlockSpec(memory_space=pl.ANY),
            pl.BlockSpec(memory_space=pltpu.VMEM),
            pl.BlockSpec(memory_space=pltpu.SMEM),
        ],
        out_specs=pl.BlockSpec(memory_space=pltpu.VMEM),
        scratch_shapes=[
            pltpu.VMEM((units, groups * rows, width), jnp.bfloat16),
            pltpu.VMEM((slots, vocab, width), jnp.bfloat16),
            pltpu.VMEM((vocab, groups * rows), jnp.float32),
            pltpu.VMEM((groups * rows // 128, 8, 128), jnp.float32),
            pltpu.VMEM((n_dev, 8, 128), jnp.float32),
            pltpu.SemaphoreType.DMA((chunks,)),
            pltpu.SemaphoreType.DMA((slots,)),
            pltpu.SemaphoreType.DMA((5, units)),
            pltpu.SemaphoreType.DMA((units,)),
            pltpu.SemaphoreType.DMA((chunks,)),
            pltpu.SemaphoreType.DMA,
            pltpu.SemaphoreType.DMA,
        ],
        compiler_params=pltpu.CompilerParams(
            collective_id=0, has_side_effects=True, vmem_limit_bytes=67_043_328),
    )(hidden.reshape(rows, part), unembed.T, targets, lengths)


def solution(mesh):
    in_specs = (P("aa", "ba", None, "col"), P(None, ("aa", "ba", "col")), P(), P())
    out_specs = P("aa", "ba")
    return jax.shard_map(body, mesh=mesh, in_specs=in_specs, out_specs=out_specs, check_vma=False)
```

profile of v0, /device:TPU:0, one launch (start us, length us, event | category | flops | bytes accessed | tf_op | source)
XLA Modules:
  0.0 69.5 jit_solution(2856125743429490381)
XLA Ops:
  0.0 68.3 %shard_map.46 = f32[1,1]{1,0:T(1,128)} custom-call(bf16[32,2048]{1,0:T(8,128)(2,1)} %bitcast.2, bf16[4752,8192]{1,0:T(8,128)(2,1)} %bitcast.1.w_ref, s32[2,4,32]{2,1,0:T(4,128)} %tgt_ref.1, s32[2,4]{1,0:T(2,128)} %len_ref.1), custom_call_target="tpu_custom_call" | custom-call | tf_op jit(solution)/shard_map/pallas_call | solution.py:242
where the time goes:
time: 69.7 us; the launch traced here: 69.5 us
  Pallas kernels  68.3 us (98%)
  between operations  1.2 us (2%)
    pallas_call x1, Pallas kernels, body(): pl.pallas_call(functools.partial(kernel, dims), out_shape=jax.ShapeDtypeS...  68.3 us

commit v1 on v0

--- a/solution.py
+++ b/solution.py
@@ -9,6 +9,17 @@
 from jax.sharding import PartitionSpec as P
 
 MESH = pl.DeviceIdType.MESH
+LINK = 0.7
+LATENCY = 1.8
+COLUMN = 2.3
+MATE = 1.1
+SHADOW = 1.5
+SLACK = 0.8
+SINGLE = 1.62
+PAIR = 2.95
+WEIGHT = 1.42
+SINGLES = 6
+FLIGHT = 4
 VMEM_BUDGET = 59 * 2**20
 Z, X, A, DIAG, SIB = range(5)
 
@@ -26,6 +37,61 @@
         value = value + on * (bit - 2 * bit * lax.rem(value // bit, 2))
         bit *= 2
     return value
+
+
+def schedule(chunks, n_c, slots, quanta):
+    units = n_c * chunks
+    ready = {(0, i): 0.0 for i in range(chunks)}
+    clock = COLUMN
+    for i in range(chunks, units):
+        clock += LINK * min(2, i // chunks)
+        ready[0, i] = clock
+    lists, now, busy, first, fed = [], 0.0, 0.0, 0, min(FLIGHT, slots)
+    for q, count in enumerate(quanta):
+        out = []
+        here = [(2, i) for i in range(first, first + count)]
+        soon = [(2, i) for i in range(first + count, first + count + quanta[min(q + 1, len(quanta) - 1)])]
+        waited = False
+        while ready:
+            key = min(ready, key=lambda key: (ready[key], -key[0], key[1]))
+            must = any(kind < 2 and (2, i) in here or (kind, i) in here for kind, i in ready)
+            ahead = any((kind, i) in soon and at < now + SLACK for (kind, i), at in ready.items())
+            if ready[key] > now and not must and not (q and ahead):
+                if waited:
+                    now += MATE if q else SHADOW
+                    waited = False
+                    continue
+                break
+            if ready[key] > now:
+                waited = waited or must
+                now = ready[key]
+            kind, i = key
+            del ready[key]
+            out.append(key)
+            if kind < 2:
+                busy = max(now, busy) + LINK / (1 + kind)
+                ready[kind + 1, i] = busy + LATENCY
+            limit = first + slots if q else min(slots, FLIGHT + int((now + 2.0) / WEIGHT))
+            while fed < min(units, limit):
+                out.append((3, fed))
+                fed += 1
+        while q and fed < min(units, first + slots):
+            out.append((3, fed))
+            fed += 1
+        lists.append(out)
+        first += count
+        now += SINGLE if count == 1 else PAIR
+    return lists
+
+
+def split(units):
+    single = min(SINGLES, units)
+    single += (units - single) % 2
+    return [1] * single + [2] * ((units - single) // 2)
+
+
+def wrap(value, count):
+    return jnp.where(value >= count, value - count, value)
 
 
 def kernel(dims, hid_ref, w_ref, tgt_ref, len_ref, out_ref, hid, wbuf, acc, stat_send, stat_recv,
@@ -40,8 +106,14 @@
     x, k = b // 2, lax.rem(b, 2)
     rank = a * n_b + b
     me = rank * n_c + c
+    flight = min(FLIGHT, slots)
+    others_a = [wrap(a + d, n_a) for d in range(1, n_a)]
+    others_x = [wrap(x + d, n_x) for d in range(1, n_x)]
+    columns = [c] + [flip(c, step, n_c) for step in range(1, n_c)]
 
     def unit_of(i):
+        if isinstance(i, int):
+            return columns[i // chunks] * chunks + i % chunks
         return flip(c, i // chunks, n_c) * chunks + lax.rem(i, chunks)
 
     def block(u, r, count=1):
@@ -70,133 +142,141 @@
         send(u, r, SIB, (a, b + 1 - 2 * k, c), plane_sem.at[u])
 
     def share(u):
-        for dx in range(1, n_x):
-            send(u, rank, X, (a, lax.rem(x + dx, n_x) * 2 + k, c), plane_sem.at[u])
-        for da in range(1, n_a):
-            send(u, rank, A, (lax.rem(a + da, n_a), b, c), plane_sem.at[u])
+        for ox in others_x:
+            send(u, rank, X, (a, ox * 2 + k, c), plane_sem.at[u])
+        for oa in others_a:
+            send(u, rank, A, (oa, b, c), plane_sem.at[u])
         to_sibling(u, rank)
 
     def stage0(i):
         u = unit_of(i)
-        await_blocks(u, Z, 1)
+        if i >= chunks:
+            await_blocks(u, Z, 1)
         share(u)
 
     def stage1(i):
         u = unit_of(i)
         await_blocks(u, X, n_x - 1)
         await_blocks(u, A, n_a - 1)
-        for da in range(1, n_a):
-            for dx in range(1, n_x):
-                step_a = lax.rem(a + da, n_a) - a
-                step_x = lax.rem(x + dx, n_x) - x
-                src = (a + step_a * (1 - k)) * n_b + (x + step_x * k) * 2 + k
-                send(u, src, DIAG, (a + step_a * k, (x + step_x * (1 - k)) * 2 + k, c), plane_sem.at[u])
-        for dx in range(1, n_x):
-            to_sibling(u, a * n_b + lax.rem(x + dx, n_x) * 2 + k)
-        for da in range(1, n_a):
-            to_sibling(u, lax.rem(a + da, n_a) * n_b + b)
+        for oa in others_a:
+            for ox in others_x:
+                src = (a + (oa - a) * (1 - k)) * n_b + (x + (ox - x) * k) * 2 + k
+                send(u, src, DIAG, (a + (oa - a) * k, (x + (ox - x) * (1 - k)) * 2 + k, c), plane_sem.at[u])
+        for ox in others_x:
+            to_sibling(u, a * n_b + ox * 2 + k)
+        for oa in others_a:
+            to_sibling(u, oa * n_b + b)
 
     def stage2(i):
         u = unit_of(i)
         await_blocks(u, DIAG, (n_a - 1) * (n_x - 1))
-        for da in range(1, n_a):
-            for dx in range(1, n_x):
-                to_sibling(u, lax.rem(a + da, n_a) * n_b + lax.rem(x + dx, n_x) * 2 + k)
-
+        for oa in others_a:
+            for ox in others_x:
+                to_sibling(u, oa * n_b + ox * 2 + k)
+
+    barrier = pltpu.get_barrier_semaphore()
+    partners = [(a, b + 1 - 2 * k, c)]
+    partners += [(a, ox * 2 + k, c) for ox in others_x]
+    partners += [(oa, b, c) for oa in others_a]
+    partners += [(a, b, oc) for oc in columns[1:]]
+    for device in partners:
+        pl.semaphore_signal(barrier, inc=1, device_id=device, device_id_type=MESH)
     for j in range(chunks):
         own(j).start()
-    for i in range(slots):
-        weights(i).start()
-
-    def other(d):
-        dev = lax.rem(me + d, n_dev)
-        group = dev // n_c
-        return (group // n_b, lax.rem(group, n_b), lax.rem(dev, n_c)), group
-
-    barrier = pltpu.get_barrier_semaphore()
-
-    @pl.loop(1, n_dev)
-    def _(d):
-        pl.semaphore_signal(barrier, inc=1, device_id=other(d)[0], device_id_type=MESH)
-
+    acc[...] = jnp.zeros_like(acc)
+    stat_send[...] = jnp.zeros_like(stat_send)
     for j in range(chunks):
         own(j).wait()
-    pl.semaphore_wait(barrier, n_dev - 1)
-
-    for j in range(chunks):
-        share(c * chunks + j)
-    for step in range(1, n_c):
+    for i in range(flight):
+        weights(i).start()
+    pl.semaphore_wait(barrier, len(partners))
+
+    def to_column(step, j):
+        send(c * chunks + j, rank, Z, (a, b, columns[step]), z_sem.at[j])
+
+    actions = (stage0, stage1, stage2, lambda i: weights(i).start())
+    quanta = split(units)
+    plan = schedule(chunks, n_c, slots, quanta)
+
+    def run(steps):
+        for kind, i in steps:
+            actions[kind](i)
+
+    own_steps, rest = plan[0][:chunks], plan[0][chunks:]
+    for j, (kind, i) in enumerate(own_steps):
+        actions[kind](i)
+        if n_c > 1:
+            to_column(1, j)
+    for step in range(2, n_c):
         for j in range(chunks):
-            u = c * chunks + j
-            send(u, rank, Z, (a, b, flip(c, step, n_c)), z_sem.at[j])
-
-    acc[...] = jnp.zeros_like(acc)
-    stat_send[...] = jnp.zeros_like(stat_send)
-
-    lead0, lead1, lead2 = 3, 2, 1
-    for i in range(lead1):
-        if i >= chunks:
-            stage0(i)
-        stage1(i)
-        if i == 0:
-            stage2(0)
-    for i in range(max(chunks, lead1), lead0):
-        stage0(i)
-
-    def accumulate(u, slot, span):
-        acc[span, :] += lax.dot_general(
-            wbuf[slot, span, :], hid[u], (((1,), (1,)), ((), ())), preferred_element_type=jnp.float32)
-
-    @pl.loop(0, units)
-    def _(i):
-        @pl.when(jnp.logical_and(i + lead0 >= chunks, i + lead0 < units))
-        def _():
-            stage0(i + lead0)
-
-        @pl.when(i + lead1 < units)
-        def _():
-            stage1(i + lead1)
-
-        @pl.when(i + lead2 < units)
-        def _():
-            stage2(i + lead2)
-
-        u = unit_of(i)
-        await_blocks(u, SIB, groups // 2)
-        weights(i).wait()
-        slot = lax.rem(i, slots)
-
-        @pl.loop(0, vocab // tile)
-        def _(n):
-            accumulate(u, slot, pl.ds(pl.multiple_of(n * tile, 8), tile))
-
-        if vocab % tile:
-            accumulate(u, slot, pl.ds(vocab // tile * tile, vocab % tile))
-
-        @pl.when(i + slots < units)
-        def _():
-            weights(i + slots).start()
-
+            to_column(step, j)
+    run(rest)
+
+    def product(first, count, span):
+        total = acc[span, :]
+        for i in range(count):
+            total += lax.dot_general(
+                wbuf[lax.rem(first + i, slots), span, :], hid[unit_of(first + i)], (((1,), (1,)), ((), ())),
+                preferred_element_type=jnp.float32)
+        return total
+
+    def arrive(first, count):
+        for i in range(count):
+            weights(first + i).wait()
+        for i in range(count):
+            await_blocks(unit_of(first + i), SIB, groups // 2)
+
+    spans = [pl.ds(n, min(tile, vocab - n)) for n in range(0, vocab, tile)]
+    begin = 0
+    for count in (1, 2):
+        start = sum(quanta[:begin])
+        number = quanta.count(count) - (count == quanta[-1])
+
+        @pl.loop(0, number)
+        def _(t, count=count, start=start, begin=begin, number=number):
+            for q in range(number):
+                if begin + q and plan[begin + q]:
+                    pl.when(t == q)(lambda q=q: run(plan[begin + q]))
+            first = start + t * count
+            arrive(first, count)
+            for span in spans:
+                acc[span, :] = product(first, count, span)
+
+        begin += number
+
+    run(plan[begin])
+    count = quanta[-1]
+    arrive(units - count, count)
     ids = jnp.concatenate(
         [tgt_ref[g // n_b, g % n_b:g % n_b + 1, :] for g in range(groups)], axis=1) - me * vocab
+    tops, totals, picks = [], [], []
+    for span in spans:
+        acc[span, :] = product(units - count, count, span)
+        part = acc[span, :]
+        top = jnp.max(part, axis=0, keepdims=True)
+        at = lax.broadcasted_iota(jnp.int32, part.shape, 0) + span.start
+        tops.append(top)
+        totals.append(jnp.sum(jnp.exp(part - top), axis=0, keepdims=True))
+        picks.append(jnp.sum(jnp.where(at == ids, part, 0.0), axis=0, keepdims=True))
+    top = functools.reduce(jnp.maximum, tops)
+    total = sum(s * jnp.exp(m - top) for s, m in zip(totals, tops))
+    picked = sum(picks)
     for t in range(groups * rows // 128):
         lanes = slice(t * 128, (t + 1) * 128)
-        part = acc[:, lanes]
-        top = jnp.max(part, axis=0, keepdims=True)
-        at = lax.broadcasted_iota(jnp.int32, part.shape, 0)
-        stat_send[t, 0:1, :] = top
-        stat_send[t, 1:2, :] = jnp.sum(jnp.exp(part - top), axis=0, keepdims=True)
-        stat_send[t, 2:3, :] = jnp.sum(jnp.where(at == ids[:, lanes], part, 0.0), axis=0, keepdims=True)
-
-    def stats(d):
-        device, group = other(d)
-        return pltpu.make_async_remote_copy(
-            src_ref=stat_send.at[group * rows // 128], dst_ref=stat_recv.at[me],
-            send_sem=stat_send_sem, recv_sem=stat_recv_sem, device_id=device, device_id_type=MESH)
-
-    @pl.loop(1, n_dev)
-    def _(d):
-        stats(d).start()
+        stat_send[t, 0:1, :] = top[:, lanes]
+        stat_send[t, 1:2, :] = total[:, lanes]
+        stat_send[t, 2:3, :] = picked[:, lanes]
+
+    all_a, all_b = [a] + others_a, [b] + [wrap(b + d, n_b) for d in range(1, n_b)]
+    for oa in reversed(all_a):
+        for ob in reversed(all_b):
+            for oc in reversed(columns):
+                if oa is a and ob is b and oc is c:
+                    continue
+                pltpu.make_async_remote_copy(
+                    src_ref=stat_send.at[(oa * n_b + ob) * rows // 128], dst_ref=stat_recv.at[me],
+                    send_sem=stat_send_sem, recv_sem=stat_recv_sem, device_id=(oa, ob, oc),
+                    device_id_type=MESH).start()
 
     stat_recv[me] = stat_send[rank * rows // 128]
 
@@ -229,7 +309,7 @@
     rows = hidden.shape[0] * hidden.shape[1] * hidden.shape[2]
     part = hidden.shape[3]
     vocab = unembed.shape[1]
-    width = math.gcd(part, 1024)
+    width = math.gcd(part, 512)
     chunks = part // width
     units = n_c * chunks
     groups = n_a * n_b

time: 69.7 us -> 47.8 us (0.69)
  Pallas kernels: 68.3 us -> 46.4 us
    pallas_call x1, Pallas kernels: 68.3 us -> 46.4 us  [body(): pl.pallas_call(functools.partial(kernel, dims), out_shape=jax.ShapeDtypeS...]
where the time goes in v1:
time: 47.8 us; the launch traced here: 47.6 us
  Pallas kernels  46.4 us (97%)
  between operations  1.2 us (3%)
    pallas_call x1, Pallas kernels, body(): pl.pallas_call(functools.partial(kernel, dims), out_shape=jax.ShapeDtypeS...  46.4 us

profile of v1, /device:TPU:0, one launch (start us, length us, event | category | flops | bytes accessed | tf_op | source)
XLA Modules:
  0.0 47.6 jit_solution(7326062244367307154)
XLA Ops:
  0.0 46.4 %shard_map.46 = f32[1,1]{1,0:T(1,128)} custom-call(bf16[32,2048]{1,0:T(8,128)(2,1)} %bitcast.2, bf16[4752,8192]{1,0:T(8,128)(2,1)} %bitcast.1.w_ref, s32[2,4,32]{2,1,0:T(4,128)} %tgt_ref.1, s32[2,4]{1,0:T(2,128)} %len_ref.1), custom_call_target="tpu_custom_call" | custom-call | tf_op jit(solution)/shard_map/pallas_call | solution.py:322

commit v2 on v1

--- a/solution.py
+++ b/solution.py
@@ -10,7 +10,7 @@
 
 MESH = pl.DeviceIdType.MESH
 LINK = 0.7
-LATENCY = 1.8
+LATENCY = 1.6
 COLUMN = 2.3
 MATE = 1.1
 SHADOW = 1.5
@@ -20,6 +20,8 @@
 WEIGHT = 1.42
 SINGLES = 6
 FLIGHT = 4
+DIRECT = 1
+HOP = 0.5
 VMEM_BUDGET = 59 * 2**20
 Z, X, A, DIAG, SIB = range(5)
 
@@ -70,7 +72,11 @@
             out.append(key)
             if kind < 2:
                 busy = max(now, busy) + LINK / (1 + kind)
-                ready[kind + 1, i] = busy + LATENCY
+                if i < DIRECT and kind == 0:
+                    busy += LINK
+                    ready[2, i] = busy + LATENCY + HOP
+                if i >= DIRECT or kind == 0:
+                    ready[kind + 1, i] = busy + LATENCY
             limit = first + slots if q else min(slots, FLIGHT + int((now + 2.0) / WEIGHT))
             while fed < min(units, limit):
                 out.append((3, fed))
@@ -148,17 +154,24 @@
             send(u, rank, A, (oa, b, c), plane_sem.at[u])
         to_sibling(u, rank)
 
+    def across(u):
+        for oa in others_a:
+            for ox in others_x:
+                send(u, rank, DIAG, (oa, ox * 2 + k, c), plane_sem.at[u])
+
     def stage0(i):
         u = unit_of(i)
         if i >= chunks:
             await_blocks(u, Z, 1)
         share(u)
+        if i < DIRECT:
+            across(u)
 
     def stage1(i):
         u = unit_of(i)
         await_blocks(u, X, n_x - 1)
         await_blocks(u, A, n_a - 1)
-        for oa in others_a:
+        for oa in others_a if i >= DIRECT else []:
             for ox in others_x:
                 src = (a + (oa - a) * (1 - k)) * n_b + (x + (ox - x) * k) * 2 + k
                 send(u, src, DIAG, (a + (oa - a) * k, (x + (ox - x) * (1 - k)) * 2 + k, c), plane_sem.at[u])
@@ -178,6 +191,7 @@
     partners = [(a, b + 1 - 2 * k, c)]
     partners += [(a, ox * 2 + k, c) for ox in others_x]
     partners += [(oa, b, c) for oa in others_a]
+    partners += [(oa, ox * 2 + k, c) for oa in others_a for ox in others_x]
     partners += [(a, b, oc) for oc in columns[1:]]
     for device in partners:
         pl.semaphore_signal(barrier, inc=1, device_id=device, device_id_type=MESH)
@@ -315,7 +329,7 @@
     groups = n_a * n_b
     n_dev = groups * n_c
     padded = round_up(vocab, 8)
-    tile = max(t for t in range(8, min(vocab, 800) + 1, 8) if vocab % 8 or vocab % t == 0)
+    tile = max(t for t in range(8, min(vocab, 528) + 1, 8) if vocab % 8 or vocab % t == 0)
     held = groups * rows * (units * width * 2 + padded * 4) + (n_dev + groups) * 4096
     slots = min(units, (VMEM_BUDGET - held) // (width * padded * 2))
     dims = (n_a, n_b, n_c, rows, width, vocab, tile, slots)

time: 47.8 us -> 46.6 us (0.975)
  Pallas kernels: 46.4 us -> 45.1 us
    pallas_call x1, Pallas kernels: 46.4 us -> 45.1 us  [body(): pl.pallas_call(functools.partial(kernel, dims), out_shape=jax.ShapeDtypeS...]
where the time goes in v2:
time: 46.6 us; the launch traced here: 46.3 us
  Pallas kernels  45.1 us (97%)
  between operations  1.2 us (3%)
    pallas_call x1, Pallas kernels, body(): pl.pallas_call(functools.partial(kernel, dims), out_shape=jax.ShapeDtypeS...  45.1 us

profile of v2, /device:TPU:0, one launch (start us, length us, event | category | flops | bytes accessed | tf_op | source)
XLA Modules:
  0.0 46.3 jit_solution(3325728534328980688)
XLA Ops:
  0.0 45.1 %shard_map.46 = f32[1,1]{1,0:T(1,128)} custom-call(bf16[32,2048]{1,0:T(8,128)(2,1)} %bitcast.2, bf16[4752,8192]{1,0:T(8,128)(2,1)} %bitcast.1.w_ref, s32[2,4,32]{2,1,0:T(4,128)} %tgt_ref.1, s32[2,4]{1,0:T(2,128)} %len_ref.1), custom_call_target="tpu_custom_call" | custom-call | tf_op jit(solution)/shard_map/pallas_call | solution.py:336
